TPU v7x, 32 devices: a whole 2x2x4 slice. The times are simulated.
32 devices in a mesh: groups: 2 (over y), rows: 4 (over z), sub: 4 (over x, core).
Axes of the slice: x: 2, y: 2, z: 4, core: 2. Of those that a mesh axis runs over, the one named last changes fastest.
Arguments:
- matrix: float32 [16384, 1024], P(('groups', 'rows', 'sub')), parts along dimension 0
- sign_bits: int32 [16384], P(('groups', 'rows', 'sub')), parts along dimension 0, may hold values from 0 to 1
- samples: int32 [8192], P('groups'), parts along dimension 0, may hold values from 0 to 8191
Outputs:
- cholesky_factor: float32 [2048, 1024], P('groups'), parts along dimension 0
There are 2 independent parts, one for each index of `groups`. A program takes and returns all parts, laid end to end along the dimension named above; each array names one. Nothing has to cross between parts.
Inputs may be any that keep to these rules, and one draw needn't show every extreme that they name: `samples`: row numbers of the whole matrix, drawn independently; a row may be drawn more than once.
All inputs are finite; a program needn't handle non-finite values.
Results may differ from a plain program's by a relative error of at most 0.00011.
Values sent between devices are 32-bit elements; how exact they have to be, the bound alone decides.
A program may use at most 64 MiB of HBM per device.

v0:
```python
import jax
import jax.numpy as jnp
from jax import lax
from jax.sharding import PartitionSpec as P

HIGHEST = lax.Precision.HIGHEST


def hadamard_table(extent):
    line_ids = jnp.arange(extent, dtype=jnp.int32)
    correlation = jnp.bitwise_and(line_ids[:, None], line_ids[None, :])
    parity = jnp.zeros((extent, extent), jnp.int32)
    for bit_pos in range(extent.bit_length() - 1):
        parity = parity + jnp.bitwise_and(jnp.right_shift(correlation, bit_pos), 1)
    return (1 - 2 * (parity % 2)).astype(jnp.float32)


def local_transform(values):
    rows_here, columns = values.shape
    inner_size = min(rows_here, 128)
    outer_size = rows_here // inner_size
    blocks = values.reshape(outer_size, inner_size, columns)
    blocks = jnp.einsum("ab,qbn->qan", hadamard_table(inner_size), blocks, precision=HIGHEST)
    blocks = jnp.einsum("pq,qan->pan", hadamard_table(outer_size), blocks, precision=HIGHEST)
    return blocks.reshape(rows_here, columns)


def mix_sources(received):
    return jnp.einsum("ab,bjn->ajn", hadamard_table(received.shape[0]), received, precision=HIGHEST)


def body(matrix, sign_bits, samples):
    rows_here, columns = matrix.shape
    devices = lax.axis_size(("rows", "sub"))
    position = lax.axis_index(("rows", "sub"))
    per_block = rows_here // devices
    sign_values = (2 * sign_bits - 1).astype(jnp.float32)
    current = local_transform(matrix * sign_values[:, None])
    block_ids = (
        (jnp.arange(devices, dtype=jnp.int32) * rows_here)[:, None]
        + position * per_block
        + jnp.arange(per_block, dtype=jnp.int32)[None, :]
    )
    blocks = current.reshape(devices, per_block, columns)
    mixed_rows = mix_sources(
        lax.all_to_all(blocks, ("rows", "sub"), split_axis=0, concat_axis=0, tiled=True)
    )
    owned_rows = mixed_rows.reshape(rows_here, columns)
    row_ids = block_ids.reshape(rows_here)
    matches = (row_ids[:, None] == samples[None, :]).astype(jnp.float32)
    counts = jnp.sum(matches, axis=1)
    weighted = owned_rows * counts[:, None]
    total_rows = rows_here * devices
    own_terms = jnp.einsum("rn,rm->nm", weighted, owned_rows, precision=HIGHEST) / jnp.float32(
        total_rows * samples.shape[0]
    )
    gram_matrix = lax.psum(own_terms, ("rows", "sub"))
    return jnp.linalg.cholesky(gram_matrix)


def solution(mesh):
    placed = (P(("groups", "rows", "sub"), None), P(("groups", "rows", "sub")), P("groups"))
    return jax.shard_map(
        body, mesh=mesh, in_specs=placed, out_specs=P("groups", None), check_vma=False
    )
```

profile of v0, /device:TPU:0, one launch (start us, length us, event | category | flops | bytes accessed | tf_op | source)
XLA Modules:
  0.0 427.4 jit_solution(5437568680601087725)
XLA Ops:
  9.0 3.5 convolution_bitcast_fusion
  14.5 5.4 %fusion.69 = f32[4,128,1024]{2,0,1:T(4,128)S(1)} fusion(f32[4,128,1024]{2,0,1:T(4,128)} %copy.23), kind=kOutput, calls=%fused_computation.112 | convolution fusion | flops 25166144 | bytes 4194304 | tf_op jit(solution)/shard_map/pq,qan->pan/dot_general | solution.py:24
  22.4 7.4 %all-to-all-start = ((f32[16,32,1024]{2,1,0:T(8,128)}), f32[16,32,1024]{2,1,0:T(8,128)S(1)}, u32[]{:S(2)}, u32[]{:S(2)}) async-start(f32[16,32,1024]{2,1,0:T(8,128)} %bitcast.60), calls=%async_computation | async-start | bytes 4194304 | tf_op jit(solution)/shard_map/all_to_all | solution.py:46
  31.4 39.4 %all-to-all-done = f32[16,32,1024]{2,1,0:T(8,128)S(1)} async-done(((f32[16,32,1024]{2,1,0:T(8,128)}), f32[16,32,1024]{2,1,0:T(8,128)S(1)}, u32[]{:S(2)}, u32[]{:S(2)}) %all-to-all-start) | async-done | bytes 2097184 | tf_op jit(solution)/shard_map/all_to_all | solution.py:46
  73.7 8.9 %bitcast_multiply_fusion = f32[1024,1024]{0,1:T(8,128)} fusion(f32[16,32,1024]{2,0,1:T(8,128)S(1)} %fusion.5, f32[16,32]{0,1:T(8,128)S(1)} %copy.26), kind=kOutput, calls=%fused_computation.3 | convolution fusion | flops 6444023808 | bytes 6293504 | tf_op jit(solution)/shard_map/rn,rm->nm/dot_general | solution.py:54
  82.6 117.7 %all-reduce.3.cloned.1.call-done = f32[1024,1024]{0,1:T(8,128)} async-done(((f32[1024,1024]{0,1:T(8,128)}), f32[1024,1024]{0,1:T(8,128)}) %all-reduce.3.cloned.1.call-update) | async-done | bytes 4194320 | tf_op jit(solution)/shard_map/psum | solution.py:57
  200.3 5.5 %copy.28 = f32[1024,1024]{1,0:T(8,128)} copy(f32[1024,1024]{0,1:T(8,128)} %all-reduce.3.cloned.1.call-done) | data formatting | bytes 8388608 | tf_op jit(solution)/shard_map/psum | solution.py:57
  205.8 4.4 %fusion = f32[1024,1024]{1,0:T(8,128)S(1)} fusion(f32[1024,1024]{1,0:T(8,128)} %copy.28, f32[1024,1024]{0,1:T(8,128)} %all-reduce.3.cloned.1.call-done), kind=kLoop, calls=%fused_computation.2 | loop fusion | flops 2097152 | bytes 12582912 | tf_op jit(solution)/shard_map/jit(cholesky)/div | solution.py:58
  212.2 11.7 %cholesky.223 = f32[128,128]{1,0:T(8,128)S(1)} custom-call(f32[128,128]{1,0:T(8,128)S(1)} %cholesky.580), custom_call_target="Cholesky" | custom-call | tf_op jit(solution)/shard_map/jit(cholesky)/cholesky | solution.py:58
  224.0 9.8 %custom-call.59 = f32[1,128,128]{1,2,0:T(8,128)S(1)} custom-call(f32[1,128,128]{2,1,0:T(8,128)S(1)} %get-tuple-element.26), custom_call_target="InvertDiagBlocksLowerTriangular" | custom-call | tf_op jit(solution)/shard_map/jit(cholesky)/cholesky | solution.py:58
  240.2 12.1 %cholesky.244 = f32[128,128]{1,0:T(8,128)S(1)} custom-call(f32[128,128]{1,0:T(8,128)S(1)} %cholesky.584), custom_call_target="Cholesky" | custom-call | tf_op jit(solution)/shard_map/jit(cholesky)/cholesky | solution.py:58
  252.9 9.8 %custom-call.60 = f32[1,128,128]{1,2,0:T(8,128)S(1)} custom-call(f32[1,128,128]{2,1,0:T(8,128)S(1)} %get-tuple-element.23), custom_call_target="InvertDiagBlocksLowerTriangular" | custom-call | tf_op jit(solution)/shard_map/jit(cholesky)/cholesky | solution.py:58
  266.1 11.7 %cholesky.468 = f32[128,128]{1,0:T(8,128)S(1)} custom-call(f32[128,128]{1,0:T(8,128)S(1)} %cholesky.589), custom_call_target="Cholesky" | custom-call | tf_op jit(solution)/shard_map/jit(cholesky)/cholesky | solution.py:58
  279.1 9.8 %custom-call.61 = f32[1,128,128]{1,2,0:T(8,128)S(1)} custom-call(f32[1,128,128]{2,1,0:T(8,128)S(1)} %get-tuple-element.20), custom_call_target="InvertDiagBlocksLowerTriangular" | custom-call | tf_op jit(solution)/shard_map/jit(cholesky)/cholesky | solution.py:58
  292.4 11.8 %cholesky.487 = f32[128,128]{1,0:T(8,128)S(1)} custom-call(f32[128,128]{1,0:T(8,128)S(1)} %cholesky.594), custom_call_target="Cholesky" | custom-call | tf_op jit(solution)/shard_map/jit(cholesky)/cholesky | solution.py:58
  305.5 9.8 %custom-call.62 = f32[1,128,128]{1,2,0:T(8,128)S(1)} custom-call(f32[1,128,128]{2,1,0:T(8,128)S(1)} %get-tuple-element.17), custom_call_target="InvertDiagBlocksLowerTriangular" | custom-call | tf_op jit(solution)/shard_map/jit(cholesky)/cholesky | solution.py:58
  318.8 11.7 %cholesky.506 = f32[128,128]{1,0:T(8,128)S(1)} custom-call(f32[128,128]{1,0:T(8,128)S(1)} %cholesky.599), custom_call_target="Cholesky" | custom-call | tf_op jit(solution)/shard_map/jit(cholesky)/cholesky | solution.py:58
  331.8 10.0 %custom-call.63 = f32[1,128,128]{1,2,0:T(8,128)S(1)} custom-call(f32[1,128,128]{2,1,0:T(8,128)S(1)} %get-tuple-element.14), custom_call_target="InvertDiagBlocksLowerTriangular" | custom-call | tf_op jit(solution)/shard_map/jit(cholesky)/cholesky | solution.py:58
  345.1 11.7 %cholesky.526 = f32[128,128]{1,0:T(8,128)S(1)} custom-call(f32[128,128]{1,0:T(8,128)S(1)} %cholesky.604), custom_call_target="Cholesky" | custom-call | tf_op jit(solution)/shard_map/jit(cholesky)/cholesky | solution.py:58
  358.1 9.8 %custom-call.64 = f32[1,128,128]{1,2,0:T(8,128)S(1)} custom-call(f32[1,128,128]{2,1,0:T(8,128)S(1)} %get-tuple-element.11), custom_call_target="InvertDiagBlocksLowerTriangular" | custom-call | tf_op jit(solution)/shard_map/jit(cholesky)/cholesky | solution.py:58
  371.0 11.9 %cholesky.546 = f32[128,128]{1,0:T(8,128)S(1)} custom-call(f32[128,128]{1,0:T(8,128)S(1)} %cholesky.609), custom_call_target="Cholesky" | custom-call | tf_op jit(solution)/shard_map/jit(cholesky)/cholesky | solution.py:58
  384.2 9.8 %custom-call.65 = f32[1,128,128]{1,2,0:T(8,128)S(1)} custom-call(f32[1,128,128]{2,1,0:T(8,128)S(1)} %get-tuple-element.8), custom_call_target="InvertDiagBlocksLowerTriangular" | custom-call | tf_op jit(solution)/shard_map/jit(cholesky)/cholesky | solution.py:58
  396.6 11.7 %cholesky.564 = f32[128,128]{1,0:T(8,128)S(1)} custom-call(f32[128,128]{1,0:T(8,128)S(1)} %convolution_subtract_fusion.6), custom_call_target="Cholesky" | custom-call | tf_op jit(solution)/shard_map/jit(cholesky)/cholesky | solution.py:58
  415.3 4.9 %select_select_fusion = f32[1024,1024]{1,0:T(8,128)} fusion(f32[1024,1024]{1,0:T(8,128)} %get-tuple-element.6, pred[]{:T(512)S(6)} %cholesky.579), kind=kLoop, calls=%fused_computation.4 | loop fusion | flops 3145728 | bytes 8388609 | tf_op jit(solution)/shard_map/jit(cholesky)/select_n | solution.py:58
  (54 shorter events, 48.0 us)
Async XLA Ops:
  19.9 10.3 %copy-start.1 = (s32[4096]{0:T(1024)S(1)}, s32[4096]{0:T(1024)}, u32[]{:S(2)}) copy-start(s32[4096]{0:T(1024)} %param.5) | copy-start | bytes 49156
  22.4 48.4 %all-to-all-start = ((f32[16,32,1024]{2,1,0:T(8,128)}), f32[16,32,1024]{2,1,0:T(8,128)S(1)}, u32[]{:S(2)}, u32[]{:S(2)}) async-start(f32[16,32,1024]{2,1,0:T(8,128)} %bitcast.60), calls=%async_computation | async-start | bytes 4194304 | tf_op jit(solution)/shard_map/all_to_all | solution.py:46
  29.8 170.5 %all-reduce.3.cloned.1.call-start = ((), (), s32[]{:S(2)}) async-start(), calls=%async_computation.1 | async-start | bytes 8388608 | tf_op jit(solution)/shard_map/psum | solution.py:57
  210.3 1.9 copy-start
Sparse Core Ops, SparseCore 0:
  82.7 117.5 all-reduce.2
where the time goes:
time: 435 us; the launch traced here: 427 us
  other arithmetic  185 us (43%)
  waiting for transfers between devices  157 us (36%)
  matrix products  43.6 us (10%)
  between operations  19 us (4%)
  local copies, waits for them, and re-layouts  14.8 us (3%)
  starting transfers between devices  7.6 us (2%)
    another operation x30, other arithmetic, body(): return jnp.linalg.cholesky(gram_matrix)  172 us
    psum x1, waiting for transfers between devices, body(): gram_matrix = lax.psum(own_terms, ('rows', 'sub'))  118 us
    all_to_all x1, waiting for transfers between devices, body(): lax.all_to_all(blocks, ('rows', 'sub'), split_axis=0, concat_axis=0, tile...  39.4 us
    another operation x14, matrix products, body(): return jnp.linalg.cholesky(gram_matrix)  22.9 us
    dot_general x1, matrix products, body(): jnp.einsum('rn,rm->nm', weighted, owned_rows, precision=HIGHEST)  8.89 us
  transfers between devices with their start and end apart: 2, of which 2 were waited for; matrix products, arithmetic and copies ran while one was open for 0% of the time, Pallas kernels for 0%

commit v1 on v0

--- a/solution.py
+++ b/solution.py
@@ -1,9 +1,105 @@
 import jax
 import jax.numpy as jnp
 from jax import lax
+from jax.experimental import pallas as pl
+from jax.experimental.pallas import tpu as pltpu
 from jax.sharding import PartitionSpec as P
 
 HIGHEST = lax.Precision.HIGHEST
+
+
+T = 128
+NT = (((1,), (1,)), ((), ()))
+NN = (((1,), (0,)), ((), ()))
+
+def factor_block(a_ref, u_ref):
+    sub8 = lax.broadcasted_iota(jnp.int32, (8, T), 0)
+    for r0 in range(0, T, 8):
+        p = a_ref[r0:r0 + 8, :]
+        left = p[:, :T]
+        cols = [jnp.broadcast_to(left[:, r0 + j:r0 + j + 1], (8, T)) for j in range(8)]
+        s = [[jnp.broadcast_to(cols[j][i:i + 1, :], (8, T)) if i <= j else None for j in range(8)] for i in range(8)]
+        fwd = [p[:, :T], p[:, T:]]
+        full = list(fwd)
+        pivots = None
+        for j in range(8):
+            d = s[j][j]
+            inv = 1.0 / d
+            pivots = d if pivots is None else jnp.where(sub8 == j, d, pivots)
+            t = [None if k <= j else s[j][k] * inv for k in range(8)]
+            m = [s[i][j] if i <= j else s[j][i] for i in range(8)]
+            mcol = m[0]
+            for i in range(1, 8):
+                mcol = jnp.where(sub8 == i, m[i], mcol)
+            for k in range(j + 1, 8):
+                for i in range(k + 1):
+                    if i != j:
+                        s[i][k] = s[i][k] - m[i] * t[k]
+                s[j][k] = t[k]
+            below = jnp.where(sub8 > j, mcol, 0.0)
+            for h in range(2):
+                frow = jnp.broadcast_to(fwd[h][j:j + 1, :], (8, T)) * inv
+                fwd[h] = fwd[h] - below * frow
+                grow = jnp.broadcast_to(full[h][j:j + 1, :], (8, T)) * inv
+                full[h] = jnp.where(sub8 == j, grow, full[h] - mcol * grow)
+        scale = lax.rsqrt(pivots)
+        for h in range(2):
+            u_ref[r0:r0 + 8, h * T:(h + 1) * T] = fwd[h] * scale
+        if r0 + 8 < T:
+            z = jnp.concatenate(full, axis=1)
+            parts = []
+            if r0:
+                parts.append(jnp.zeros((r0, 2 * T), jnp.float32))
+            parts.append(z)
+            parts.append(jnp.zeros((T - r0 - 8, 2 * T), jnp.float32))
+            z = jnp.concatenate(parts, axis=0)
+            rest = a_ref[r0 + 8:, :]
+            a_ref[r0 + 8:, :] = rest - lax.dot_general(rest[:, :T], z, NN, precision=HIGHEST, preferred_element_type=jnp.float32)
+
+def chol_kernel(g_ref, out_ref, a_ref, u_ref):
+    n = g_ref.shape[0]
+    steps = n // T
+    row = lax.broadcasted_iota(jnp.int32, (T, T), 0)
+    col = lax.broadcasted_iota(jnp.int32, (T, T), 1)
+    eye = (row == col).astype(jnp.float32)
+    for k in range(steps - 1):
+        out_ref[k * T:(k + 1) * T, (k + 1) * T:] = jnp.zeros((T, n - (k + 1) * T), jnp.float32)
+
+    def panel(k, carry):
+        here = pl.ds(pl.multiple_of(k * T, T), T)
+        a_ref[:, :T] = g_ref[here, here]
+        a_ref[:, T:] = eye
+        factor_block(a_ref, u_ref)
+        out_ref[here, here] = jnp.where(row >= col, u_ref[:, :T].T, 0.0)
+        for kk in range(steps - 1):
+            @pl.when(k == kk)
+            def _():
+                c = slice(kk * T, (kk + 1) * T)
+                lo = (kk + 1) * T
+                solved = lax.dot_general(g_ref[lo:, c], u_ref[:, T:], NT, precision=HIGHEST, preferred_element_type=jnp.float32)
+                out_ref[lo:, c] = solved
+                for j in range(kk + 1, steps):
+                    b = slice(j * T, (j + 1) * T)
+                    g_ref[j * T:, b] = g_ref[j * T:, b] - lax.dot_general(
+                        out_ref[j * T:, c], out_ref[b, c], NT, precision=HIGHEST, preferred_element_type=jnp.float32)
+        return carry
+    lax.fori_loop(0, steps, panel, 0)
+
+def chol_whole(g_in, o_ref, g_ref, a_ref, u_ref, sem):
+    cp = pltpu.make_async_copy(g_in, g_ref, sem)
+    cp.start(); cp.wait()
+    chol_kernel(g_ref, o_ref, a_ref, u_ref)
+
+def cholesky(g):
+    n = g.shape[0]
+    return pl.pallas_call(
+        chol_whole,
+        out_shape=jax.ShapeDtypeStruct((n, n), jnp.float32),
+        in_specs=[pl.BlockSpec(memory_space=pl.ANY)],
+        out_specs=pl.BlockSpec(memory_space=pltpu.VMEM),
+        scratch_shapes=[pltpu.VMEM((n, n), jnp.float32), pltpu.VMEM((T, 2 * T), jnp.float32), pltpu.VMEM((T, 2 * T), jnp.float32), pltpu.SemaphoreType.DMA],
+        compiler_params=pltpu.CompilerParams(vmem_limit_bytes=40 * 2**20),
+    )(g)
 
 
 def hadamard_table(extent):
@@ -55,7 +151,7 @@
         total_rows * samples.shape[0]
     )
     gram_matrix = lax.psum(own_terms, ("rows", "sub"))
-    return jnp.linalg.cholesky(gram_matrix)
+    return cholesky(gram_matrix)
 
 
 def solution(mesh):

time: 435 us -> 273 us (0.63); the launches traced: 427 us -> 273 us
  other arithmetic: 185 us -> 3.56 us
  Pallas kernels: 0 us -> 63.7 us
  matrix products: 43.6 us -> 20.2 us
  local copies, waits for them, and re-layouts: 14.8 us -> 6.93 us
  between operations: 19 us -> 13.5 us
    another operation x30 -> x0, other arithmetic: 172 us -> none  [body(): return jnp.linalg.cholesky(gram_matrix)]
    pallas_call x0 -> x1, Pallas kernels: none -> 63.7 us  [cholesky(): pl.pallas_call(chol_whole, out_shape=jax.ShapeDtypeStruct((n, n), jnp.flo...]
    another operation x14 -> x0, matrix products: 22.9 us -> none  [body(): return jnp.linalg.cholesky(gram_matrix)]
    psum x1 -> x0, local copies, waits for them, and re-layouts: 5.53 us -> none  [body(): gram_matrix = lax.psum(own_terms, ('rows', 'sub'))]
    select_n x1 -> x0, other arithmetic: 4.86 us -> none  [body(): return jnp.linalg.cholesky(gram_matrix)]
    div x1 -> x0, other arithmetic: 4.43 us -> none  [body(): return jnp.linalg.cholesky(gram_matrix)]
where the time goes in v1:
time: 273 us
  waiting for transfers between devices  157 us (58%)
  Pallas kernels  63.7 us (23%)
  matrix products  20.2 us (7%)
  between operations  13.5 us (5%)
  starting transfers between devices  7.74 us (3%)
  local copies, waits for them, and re-layouts  6.93 us (3%)
  other arithmetic  3.56 us (1%)
    psum x1, waiting for transfers between devices, body(): gram_matrix = lax.psum(own_terms, ('rows', 'sub'))  118 us
    pallas_call x1, Pallas kernels, cholesky(): pl.pallas_call(chol_whole, out_shape=jax.ShapeDtypeStruct((n, n), jnp.flo...  63.7 us
    all_to_all x1, waiting for transfers between devices, body(): lax.all_to_all(blocks, ('rows', 'sub'), split_axis=0, concat_axis=0, tile...  39.4 us
    dot_general x1, matrix products, body(): jnp.einsum('rn,rm->nm', weighted, owned_rows, precision=HIGHEST)  8.51 us
    all_to_all x1, starting transfers between devices, body(): lax.all_to_all(blocks, ('rows', 'sub'), split_axis=0, concat_axis=0, tile...  7.52 us
  transfers between devices with their start and end apart: 2, of which 2 were waited for; matrix products, arithmetic and copies ran while one was open for 0% of the time, Pallas kernels for 0%

profile of v1, /device:TPU:0, one launch (start us, length us, event | category | flops | bytes accessed | tf_op | source)
XLA Modules:
  0.0 272.9 jit_solution(7328613482864387673)
XLA Ops:
  6.5 0.7 add_convert_fusion
  7.2 1.8 broadcast_multiply_fusion
  9.0 3.5 %convolution_bitcast_fusion = f32[4,128,1024]{1,2,0:T(8,128)S(1)} fusion(f32[4,128,1024]{2,1,0:T(8,128)S(1)} %bitcast.19), kind=kOutput, calls=%fused_computation.6 | convolution fusion | flops 805879808 | bytes 4194304 | tf_op jit(solution)/shard_map/ab,qbn->qan/dot_general | solution.py:119
  12.5 2.0 copy.17
  14.5 5.4 %fusion.41 = f32[4,128,1024]{2,0,1:T(4,128)S(1)} fusion(f32[4,128,1024]{2,0,1:T(4,128)} %copy.17), kind=kOutput, calls=%fused_computation.51 | convolution fusion | flops 25166144 | bytes 4194304 | tf_op jit(solution)/shard_map/pq,qan->pan/dot_general | solution.py:120
  19.9 2.5 copy.18
  22.4 0.0 copy-start.1
  22.4 7.5 %all-to-all-start = ((f32[16,32,1024]{2,1,0:T(8,128)}), f32[16,32,1024]{2,1,0:T(8,128)S(1)}, u32[]{:S(2)}, u32[]{:S(2)}) async-start(f32[16,32,1024]{2,1,0:T(8,128)} %bitcast.18), calls=%async_computation | async-start | bytes 4194304 | tf_op jit(solution)/shard_map/all_to_all | solution.py:142
  29.9 0.2 all-reduce.2.cloned.1.call-start
  30.2 0.1 iota_add_fusion
  30.3 0.1 add.104
  30.3 0.0 copy-done.1
  30.3 1.0 convert_reduce_fusion
  31.4 0.1 mul.57
  31.4 0.1 copy.20
  31.5 39.4 %all-to-all-done = f32[16,32,1024]{2,1,0:T(8,128)S(1)} async-done(((f32[16,32,1024]{2,1,0:T(8,128)}), f32[16,32,1024]{2,1,0:T(8,128)S(1)}, u32[]{:S(2)}, u32[]{:S(2)}) %all-to-all-start) | async-done | bytes 2097184 | tf_op jit(solution)/shard_map/all_to_all | solution.py:142
  70.9 2.9 %fusion.4 = f32[16,32,1024]{2,0,1:T(8,128)S(1)} fusion(f32[16,32,1024]{2,1,0:T(8,128)S(1)} %all-to-all-done), kind=kOutput, calls=%fused_computation.4 | convolution fusion | flops 100669952 | bytes 4194304 | tf_op jit(solution)/shard_map/ab,bjn->ajn/dot_general | solution.py:125
  73.8 8.5 %bitcast_multiply_fusion = f32[1024,1024]{1,0:T(8,128)} fusion(f32[16,32,1024]{2,0,1:T(8,128)S(1)} %fusion.4, f32[16,32]{0,1:T(8,128)S(1)} %copy.20), kind=kOutput, calls=%fused_computation.1 | convolution fusion | flops 6444023808 | bytes 6293504 | tf_op jit(solution)/shard_map/rn,rm->nm/dot_general | solution.py:150
  82.3 0.0 all-reduce.2.cloned.1.call-update
  82.3 117.8 %all-reduce.2.cloned.1.call-done.g_in = f32[1024,1024]{1,0:T(8,128)} async-done(((f32[1024,1024]{1,0:T(8,128)}), f32[1024,1024]{1,0:T(8,128)}) %all-reduce.2.cloned.1.call-update) | async-done | bytes 4194320 | tf_op jit(solution)/shard_map/psum | solution.py:153
  200.1 0.0 copy-start
  200.1 2.2 copy-done
  202.3 63.7 %shard_map.37 = f32[1024,1024]{1,0:T(8,128)} custom-call(f32[1024,1024]{1,0:T(8,128)S(1)} %copy-done), custom_call_target="tpu_custom_call" | custom-call | tf_op jit(solution)/shard_map/pallas_call | solution.py:95
  (1 shorter events, 0.0 us)
Async XLA Ops:
  22.4 7.9 %copy-start.1 = (s32[4096]{0:T(1024)S(1)}, s32[4096]{0:T(1024)}, u32[]{:S(2)}) copy-start(s32[4096]{0:T(1024)} %param.5) | copy-start | bytes 49156
  22.4 48.5 %all-to-all-start = ((f32[16,32,1024]{2,1,0:T(8,128)}), f32[16,32,1024]{2,1,0:T(8,128)S(1)}, u32[]{:S(2)}, u32[]{:S(2)}) async-start(f32[16,32,1024]{2,1,0:T(8,128)} %bitcast.18), calls=%async_computation | async-start | bytes 4194304 | tf_op jit(solution)/shard_map/all_to_all | solution.py:142
  29.9 170.2 %all-reduce.2.cloned.1.call-start = ((), (), s32[]{:S(2)}) async-start(), calls=%async_computation.1 | async-start | bytes 8388608 | tf_op jit(solution)/shard_map/psum | solution.py:153
  200.1 2.2 copy-start
Sparse Core Ops, SparseCore 0:
  82.4 117.6 all-reduce.1

commit v2 on v1

v2 whole, which is shorter than its diff:
```python
import functools

import jax
import jax.numpy as jnp
from jax import lax
from jax.experimental import pallas as pl
from jax.experimental.pallas import tpu as pltpu
from jax.sharding import PartitionSpec as P

HIGHEST = lax.Precision.HIGHEST
VMEM = pl.BlockSpec(memory_space=pltpu.VMEM)
T = 128
NT = (((1,), (1,)), ((), ()))
NN = (((1,), (0,)), ((), ()))

def factor_block(a_ref, u_ref):
    sub8 = lax.broadcasted_iota(jnp.int32, (8, T), 0)
    for r0 in range(0, T, 8):
        p = a_ref[r0:r0 + 8, :]
        left = p[:, :T]
        cols = [jnp.broadcast_to(left[:, r0 + j:r0 + j + 1], (8, T)) for j in range(8)]
        s = [[jnp.broadcast_to(cols[j][i:i + 1, :], (8, T)) if i <= j else None for j in range(8)] for i in range(8)]
        fwd = [p[:, :T], p[:, T:]]
        full = list(fwd)
        pivots = None
        for j in range(8):
            d = s[j][j]
            inv = 1.0 / d
            pivots = d if pivots is None else jnp.where(sub8 == j, d, pivots)
            t = [None if k <= j else s[j][k] * inv for k in range(8)]
            m = [s[i][j] if i <= j else s[j][i] for i in range(8)]
            mcol = m[0]
            for i in range(1, 8):
                mcol = jnp.where(sub8 == i, m[i], mcol)
            for k in range(j + 1, 8):
                for i in range(k + 1):
                    if i != j:
                        s[i][k] = s[i][k] - m[i] * t[k]
                s[j][k] = t[k]
            below = jnp.where(sub8 > j, mcol, 0.0)
            for h in range(2):
                frow = jnp.broadcast_to(fwd[h][j:j + 1, :], (8, T)) * inv
                fwd[h] = fwd[h] - below * frow
                grow = jnp.broadcast_to(full[h][j:j + 1, :], (8, T)) * inv
                full[h] = jnp.where(sub8 == j, grow, full[h] - mcol * grow)
        scale = lax.rsqrt(pivots)
        for h in range(2):
            u_ref[r0:r0 + 8, h * T:(h + 1) * T] = fwd[h] * scale
        if r0 + 8 < T:
            z = jnp.concatenate(full, axis=1)
            parts = []
            if r0:
                parts.append(jnp.zeros((r0, 2 * T), jnp.float32))
            parts.append(z)
            parts.append(jnp.zeros((T - r0 - 8, 2 * T), jnp.float32))
            z = jnp.concatenate(parts, axis=0)
            rest = a_ref[r0 + 8:, :]
            a_ref[r0 + 8:, :] = rest - lax.dot_general(rest[:, :T], z, NN, precision=HIGHEST, preferred_element_type=jnp.float32)


def panel_start(j, steps):
    return T * (j * steps - j * (j - 1) // 2)


def chol_kernel(g_in, out_ref, g_ref, a_ref, u_ref, sem):
    n = out_ref.shape[0]
    steps = n // T
    copy = pltpu.make_async_copy(g_in, g_ref, sem)
    copy.start()
    row = lax.broadcasted_iota(jnp.int32, (T, T), 0)
    col = lax.broadcasted_iota(jnp.int32, (T, T), 1)
    eye = (row == col).astype(jnp.float32)
    for k in range(steps - 1):
        out_ref[k * T:(k + 1) * T, (k + 1) * T:] = jnp.zeros((T, n - (k + 1) * T), jnp.float32)
    copy.wait()

    def panel(k, carry):
        here = pl.ds(pl.multiple_of(k * T, T), T)
        a_ref[:, :T] = g_ref[pl.ds(pl.multiple_of(panel_start(k, steps), T), T), :]
        a_ref[:, T:] = eye
        factor_block(a_ref, u_ref)
        out_ref[here, here] = jnp.where(row >= col, u_ref[:, :T].T, 0.0)
        for kk in range(steps - 1):
            @pl.when(k == kk)
            def _():
                c = slice(kk * T, (kk + 1) * T)
                lo = (kk + 1) * T
                start = panel_start(kk, steps)
                out_ref[lo:, c] = lax.dot_general(
                    g_ref[start + T:start + (steps - kk) * T, :], u_ref[:, T:], NT,
                    precision=HIGHEST, preferred_element_type=jnp.float32)
                for j in range(kk + 1, steps):
                    b = slice(panel_start(j, steps), panel_start(j + 1, steps))
                    g_ref[b, :] = g_ref[b, :] - lax.dot_general(
                        out_ref[j * T:, c], out_ref[j * T:(j + 1) * T, c], NT,
                        precision=HIGHEST, preferred_element_type=jnp.float32)
        return carry

    lax.fori_loop(0, steps, panel, 0)


def cholesky(packed, n):
    return pl.pallas_call(
        chol_kernel,
        out_shape=jax.ShapeDtypeStruct((n, n), jnp.float32),
        in_specs=[pl.BlockSpec(memory_space=pl.ANY)],
        out_specs=VMEM,
        scratch_shapes=[
            pltpu.VMEM(packed.shape, jnp.float32),
            pltpu.VMEM((T, 2 * T), jnp.float32),
            pltpu.VMEM((T, 2 * T), jnp.float32),
            pltpu.SemaphoreType.DMA,
        ],
        compiler_params=pltpu.CompilerParams(vmem_limit_bytes=24 * 2**20),
    )(packed)


def butterfly(parts):
    stride = 1
    while stride < len(parts):
        mixed = list(parts)
        for i in range(len(parts)):
            if not i & stride:
                mixed[i] = parts[i] + parts[i + stride]
                mixed[i + stride] = parts[i] - parts[i + stride]
        parts = mixed
        stride *= 2
    return parts


def transform_kernel(x_ref, s_ref, o_ref):
    count, inner = s_ref.shape
    i = lax.broadcasted_iota(jnp.int32, (inner, inner), 0)
    j = lax.broadcasted_iota(jnp.int32, (inner, inner), 1)
    common = i & j
    parity = jnp.zeros((inner, inner), jnp.int32)
    for bit in range(inner.bit_length() - 1):
        parity = parity ^ ((common >> bit) & 1)
    table = (1 - 2 * parity).astype(jnp.float32)
    width = x_ref.shape[1] // 4
    for c in range(4):
        cols = slice(c * width, (c + 1) * width)
        parts = [
            lax.dot_general(table * s_ref[q:q + 1, :], x_ref[q * inner:(q + 1) * inner, cols], NN,
                            precision=HIGHEST, preferred_element_type=jnp.float32)
            for q in range(count)
        ]
        for q, part in enumerate(butterfly(parts)):
            o_ref[q * inner:(q + 1) * inner, cols] = part


def gram_kernel(devices, scale, r_ref, w_ref, o_ref, x_ref, t_ref):
    rows, n = x_ref.shape
    steps = n // T
    height = rows // devices
    piece = 8 if height % 8 == 0 else height
    def mix(step, carry):
        for c in range(steps):
            cols = slice(c * T, (c + 1) * T)
            at = [pl.ds(d * height + step * piece, piece) for d in range(devices)]
            if piece == 8:
                at = [pl.ds(pl.multiple_of(d * height + step * piece, 8), 8) for d in range(devices)]
            for ref_at, part in zip(at, butterfly([r_ref[a, cols] for a in at])):
                x_ref[ref_at, cols] = part
        return carry
    lax.fori_loop(0, height // piece, mix, 0)
    for c in range(steps):
        cols = slice(c * T, (c + 1) * T)
        t_ref[cols, :] = x_ref[:, cols].T * (w_ref[...] * scale)
    for j in range(steps):
        start, stop = panel_start(j, steps), panel_start(j + 1, steps)
        o_ref[start:stop, :] = lax.dot_general(
            t_ref[j * T:, :], x_ref[:, j * T:(j + 1) * T], NN,
            precision=HIGHEST, preferred_element_type=jnp.float32)
    used = panel_start(steps, steps)
    if used < o_ref.shape[0]:
        o_ref[used:, :] = jnp.zeros((o_ref.shape[0] - used, T), jnp.float32)


def gram_panels(received, counts, devices, scale, padded):
    rows, n = received.shape
    if (rows // devices) % 8:
        received = jnp.einsum("ab,bjn->ajn", hadamard_table(devices),
                              received.reshape(devices, rows // devices, n), precision=HIGHEST).reshape(rows, n)
        mixers = 1
    else:
        mixers = devices
    return pl.pallas_call(
        functools.partial(gram_kernel, mixers, scale),
        out_shape=jax.ShapeDtypeStruct((padded, T), jnp.float32),
        in_specs=[VMEM, VMEM],
        out_specs=VMEM,
        scratch_shapes=[pltpu.VMEM((rows, n), jnp.float32), pltpu.VMEM((n, rows), jnp.float32)],
        compiler_params=pltpu.CompilerParams(vmem_limit_bytes=32 * 2**20),
    )(received, counts)


def reduce_kernel(orders, rows_of_part, in_ref, out_ref, sum_ref, got_ref, send_sems, recv_sems):
    rows_id, sub_id, group_id = lax.axis_index("rows"), lax.axis_index("sub"), lax.axis_index("groups")

    def partner(axis, bit):
        mine = rows_id if axis == "rows" else sub_id
        low = lax.rem(mine // bit, 2)
        other = mine + bit * (1 - 2 * low)
        ids = (group_id, other, sub_id) if axis == "rows" else (group_id, rows_id, other)
        return low, ids

    barrier = pltpu.get_barrier_semaphore()
    for axis, bit in orders[0]:
        pl.semaphore_signal(barrier, inc=1, device_id=partner(axis, bit)[1], device_id_type=pl.DeviceIdType.MESH)
    pl.semaphore_wait(barrier, len(orders[0]))

    levels = len(orders[0])
    offsets = [[p * rows_of_part] for p in range(len(orders))]
    size = rows_of_part
    got_at = 0
    for level in range(levels):
        half = size // 2
        sent = []
        for p, order in enumerate(orders):
            low, ids = partner(*order[level])
            base = offsets[p][-1]
            keep = pl.multiple_of(base + low * half, 8)
            give = pl.multiple_of(base + (1 - low) * half, 8)
            slot = got_at + p * half
            source = in_ref if level == 0 else sum_ref
            copy = pltpu.make_async_remote_copy(
                src_ref=source.at[pl.ds(give, half)], dst_ref=got_ref.at[slot:slot + half],
                send_sem=send_sems.at[level, p], recv_sem=recv_sems.at[level, p],
                device_id=ids, device_id_type=pl.DeviceIdType.MESH)
            copy.start()
            sent.append((copy, keep, slot))
            offsets[p].append(keep)
        for copy, keep, slot in sent:
            copy.wait()
            source = in_ref if level == 0 else sum_ref
            target = out_ref if level == levels - 1 else sum_ref
            target[pl.ds(keep, half), :] = source[pl.ds(keep, half), :] + got_ref[slot:slot + half, :]
        got_at += half * len(orders)
        size = half
    for level in range(levels - 1, -1, -1):
        sent = []
        for p, order in enumerate(orders):
            low, ids = partner(*order[level])
            region = pl.ds(offsets[p][level + 1], size)
            copy = pltpu.make_async_remote_copy(
                src_ref=out_ref.at[region], dst_ref=out_ref.at[region],
                send_sem=send_sems.at[levels + level, p], recv_sem=recv_sems.at[levels + level, p],
                device_id=ids, device_id_type=pl.DeviceIdType.MESH)
            copy.start()
            sent.append(copy)
        for copy in sent:
            copy.wait()
        size *= 2


def all_reduce(panels, mesh_sizes):
    sub_bits = [("sub", 1 << b) for b in range(mesh_sizes["sub"].bit_length() - 1)]
    row_bits = [("rows", 1 << b) for b in range(mesh_sizes["rows"].bit_length() - 1)]
    orders = (tuple(sub_bits + row_bits), tuple(sub_bits[:1] + row_bits + sub_bits[1:]))
    levels = len(orders[0])
    rows = panels.shape[0]
    return pl.pallas_call(
        functools.partial(reduce_kernel, orders, rows // 2),
        out_shape=jax.ShapeDtypeStruct(panels.shape, jnp.float32),
        in_specs=[VMEM],
        out_specs=VMEM,
        scratch_shapes=[
            pltpu.VMEM(panels.shape, jnp.float32),
            pltpu.VMEM(panels.shape, jnp.float32),
            pltpu.SemaphoreType.DMA((2 * levels, 2)),
            pltpu.SemaphoreType.DMA((2 * levels, 2)),
        ],
        compiler_params=pltpu.CompilerParams(
            collective_id=0, has_side_effects=True, vmem_limit_bytes=24 * 2**20),
    )(panels)


def hadamard_table(extent):
    line_ids = jnp.arange(extent, dtype=jnp.int32)
    correlation = jnp.bitwise_and(line_ids[:, None], line_ids[None, :])
    parity = jnp.zeros((extent, extent), jnp.int32)
    for bit_pos in range(extent.bit_length() - 1):
        parity = parity + jnp.bitwise_and(jnp.right_shift(correlation, bit_pos), 1)
    return (1 - 2 * (parity % 2)).astype(jnp.float32)


def body(mesh_sizes, matrix, sign_bits, samples):
    rows_here, columns = matrix.shape
    devices = mesh_sizes["rows"] * mesh_sizes["sub"]
    position = lax.axis_index(("rows", "sub"))
    per_block = rows_here // devices
    inner = min(rows_here, 128)
    signs = (2 * sign_bits - 1).astype(jnp.float32).reshape(rows_here // inner, inner)
    current = pl.pallas_call(
        transform_kernel,
        out_shape=jax.ShapeDtypeStruct(matrix.shape, jnp.float32),
        in_specs=[VMEM, VMEM],
        out_specs=VMEM,
        compiler_params=pltpu.CompilerParams(vmem_limit_bytes=24 * 2**20),
    )(matrix, signs)
    blocks = current.reshape(devices, per_block, columns)
    received = lax.all_to_all(blocks, ("rows", "sub"), split_axis=0, concat_axis=0, tiled=True)
    line = jnp.arange(rows_here, dtype=jnp.int32)
    row_ids = (line // per_block) * rows_here + position * per_block + line % per_block
    counts = jnp.sum((row_ids[:, None] == samples[None, :]).astype(jnp.float32), axis=1)
    total_rows = rows_here * devices
    scale = 1.0 / (total_rows * samples.shape[0])
    steps = columns // T
    unit = 16 * devices
    padded = -(-panel_start(steps, steps) // unit) * unit
    panels = gram_panels(received.reshape(rows_here, columns), counts[None, :], devices, scale, padded)
    return cholesky(all_reduce(panels, mesh_sizes), columns)


def solution(mesh):
    placed = (P(("groups", "rows", "sub"), None), P(("groups", "rows", "sub")), P("groups"))
    return jax.shard_map(
        functools.partial(body, dict(mesh.shape)), mesh=mesh, in_specs=placed, out_specs=P("groups", None),
        check_vma=False
    )
```

time: 273 us -> 180 us (0.66)
  waiting for transfers between devices: 157 us -> 39.9 us
  Pallas kernels: 63.7 us -> 128 us
  matrix products: 20.2 us -> 0 us
  between operations: 13.5 us -> 0.22 us
  local copies, waits for them, and re-layouts: 6.93 us -> 2.91 us
    psum x1 -> x0, waiting for transfers between devices: 118 us -> none  [body(): gram_matrix = lax.psum(own_terms, ('rows', 'sub'))]
    pallas_call x1 -> x4, Pallas kernels: 63.7 us -> 128 us  [the longest x1 63.5 us: cholesky(): pl.pallas_call(chol_kernel, out_shape=jax.ShapeDtypeStruct((n, n), jnp.fl...]
    dot_general x4 -> x0, matrix products: 20.2 us -> none  [the longest x1 8.51 us: body(): jnp.einsum('rn,rm->nm', weighted, owned_rows, precision=HIGHEST)]
  transfers between devices with their start and end apart: 2 -> 1, of which waited for: 2 -> 1; matrix products, arithmetic and copies ran while one was open for 0% -> 1% of each run, Pallas kernels for 0% -> 0%
where the time goes in v2:
time: 180 us
  Pallas kernels  128 us (71%)
  waiting for transfers between devices  39.9 us (22%)
  starting transfers between devices  7.52 us (4%)
  local copies, waits for them, and re-layouts  2.91 us (2%)
    pallas_call x1, Pallas kernels, cholesky(): pl.pallas_call(chol_kernel, out_shape=jax.ShapeDtypeStruct((n, n), jnp.fl...  63.5 us
    pallas_call x1, Pallas kernels, all_reduce(): pl.pallas_call(functools.partial(reduce_kernel, orders, rows // 2), out_s...  54 us
    all_to_all x1, waiting for transfers between devices, body(): lax.all_to_all(blocks, ('rows', 'sub'), split_axis=0, concat_axis=0, tile...  39.9 us
    pallas_call x1, Pallas kernels, gram_panels(): pl.pallas_call(functools.partial(gram_kernel, mixers, scale), out_shape=j...  8.16 us
    all_to_all x1, starting transfers between devices, body(): lax.all_to_all(blocks, ('rows', 'sub'), split_axis=0, concat_axis=0, tile...  7.52 us
  transfers between devices with their start and end apart: 1, of which 1 were waited for; matrix products, arithmetic and copies ran while one was open for 1% of the time, Pallas kernels for 0%

profile of v2, /device:TPU:0, one launch (start us, length us, event | category | flops | bytes accessed | tf_op | source)
XLA Modules:
  0.0 179.9 jit_solution(16693867755281416806)
XLA Ops:
  0.0 0.7 convert_bitcast_fusion.s_ref
  0.7 0.0 copy-start.1
  0.7 1.6 copy-done.1
  2.3 1.9 %shard_map.37 = f32[512,1024]{1,0:T(8,128)S(1)} custom-call(f32[512,1024]{1,0:T(8,128)S(1)} %copy-done.1, f32[4,128]{1,0:T(4,128)S(1)} %convert_bitcast_fusion.s_ref), custom_call_target="tpu_custom_call" | custom-call | tf_op jit(solution)/shard_map/pallas_call | solution.py:295
  4.2 0.0 copy-start
  4.2 1.3 copy-done
  5.5 0.0 copy-start.2
  5.5 7.5 %all-to-all-start = ((f32[16,32,1024]{2,1,0:T(8,128)}), f32[16,32,1024]{2,1,0:T(8,128)S(1)}, u32[]{:S(2)}, u32[]{:S(2)}) async-start(f32[16,32,1024]{2,1,0:T(8,128)} %bitcast.6), calls=%async_computation | async-start | bytes 4194304 | tf_op jit(solution)/shard_map/all_to_all | solution.py:303
  13.1 0.0 copy-done.2
  13.1 1.0 convert_reduce_fusion
  14.1 39.9 %all-to-all-done = f32[16,32,1024]{2,1,0:T(8,128)S(1)} async-done(((f32[16,32,1024]{2,1,0:T(8,128)}), f32[16,32,1024]{2,1,0:T(8,128)S(1)}, u32[]{:S(2)}, u32[]{:S(2)}) %all-to-all-start) | async-done | bytes 2097184 | tf_op jit(solution)/shard_map/all_to_all | solution.py:303
  54.0 8.2 %shard_map.38.in_ref = f32[4608,128]{1,0:T(8,128)S(1)} custom-call(f32[512,1024]{1,0:T(8,128)S(1)} %bitcast.5, f32[1,512]{1,0:T(1,128)S(1)} %bitcast.7), custom_call_target="tpu_custom_call" | custom-call | tf_op jit(solution)/shard_map/pallas_call | solution.py:188
  62.2 54.0 %shard_map.39.g_in = f32[4608,128]{1,0:T(8,128)S(1)} custom-call(f32[4608,128]{1,0:T(8,128)S(1)} %shard_map.38.in_ref), custom_call_target="tpu_custom_call" | custom-call | tf_op jit(solution)/shard_map/pallas_call | solution.py:263
  116.2 63.5 %shard_map.40 = f32[1024,1024]{1,0:T(8,128)} custom-call(f32[4608,128]{1,0:T(8,128)S(1)} %shard_map.39.g_in), custom_call_target="tpu_custom_call" | custom-call | tf_op jit(solution)/shard_map/pallas_call | solution.py:103
  (1 shorter events, 0.0 us)
Async XLA Ops:
  0.7 1.6 copy-start.1
  4.2 1.3 copy-start
  5.5 7.5 %copy-start.2 = (s32[4096]{0:T(1024)S(1)}, s32[4096]{0:T(1024)}, u32[]{:S(2)}) copy-start(s32[4096]{0:T(1024)} %param.5) | copy-start | bytes 49156
  5.5 48.5 %all-to-all-start = ((f32[16,32,1024]{2,1,0:T(8,128)}), f32[16,32,1024]{2,1,0:T(8,128)S(1)}, u32[]{:S(2)}, u32[]{:S(2)}) async-start(f32[16,32,1024]{2,1,0:T(8,128)} %bitcast.6), calls=%async_computation | async-start | bytes 4194304 | tf_op jit(solution)/shard_map/all_to_all | solution.py:303

commit v3 on v2

--- a/solution.py
+++ b/solution.py
@@ -15,12 +15,15 @@
 
 def factor_block(a_ref, u_ref):
     sub8 = lax.broadcasted_iota(jnp.int32, (8, T), 0)
+    p = [a_ref[0:8, :T], a_ref[0:8, T:]]
     for r0 in range(0, T, 8):
-        p = a_ref[r0:r0 + 8, :]
-        left = p[:, :T]
+        left = p[0]
+        if r0 + 8 < T:
+            after = [a_ref[r0 + 8:r0 + 16, :T], a_ref[r0 + 8:r0 + 16, T:]]
+            after_cols = [jnp.broadcast_to(after[0][:, r0 + j:r0 + j + 1], (8, T)) for j in range(8)]
         cols = [jnp.broadcast_to(left[:, r0 + j:r0 + j + 1], (8, T)) for j in range(8)]
         s = [[jnp.broadcast_to(cols[j][i:i + 1, :], (8, T)) if i <= j else None for j in range(8)] for i in range(8)]
-        fwd = [p[:, :T], p[:, T:]]
+        fwd = list(p)
         full = list(fwd)
         pivots = None
         for j in range(8):
@@ -37,16 +40,19 @@
                     if i != j:
                         s[i][k] = s[i][k] - m[i] * t[k]
                 s[j][k] = t[k]
-            below = jnp.where(sub8 > j, mcol, 0.0)
             for h in range(2):
-                frow = jnp.broadcast_to(fwd[h][j:j + 1, :], (8, T)) * inv
-                fwd[h] = fwd[h] - below * frow
+                fwd[h] = jnp.where(sub8 == j, full[h], fwd[h])
                 grow = jnp.broadcast_to(full[h][j:j + 1, :], (8, T)) * inv
                 full[h] = jnp.where(sub8 == j, grow, full[h] - mcol * grow)
         scale = lax.rsqrt(pivots)
         for h in range(2):
             u_ref[r0:r0 + 8, h * T:(h + 1) * T] = fwd[h] * scale
         if r0 + 8 < T:
+            for j in range(8):
+                for h in range(2):
+                    after[h] = after[h] - after_cols[j] * jnp.broadcast_to(full[h][j:j + 1, :], (8, T))
+            p = after
+        if r0 + 16 < T:
             z = jnp.concatenate(full, axis=1)
             parts = []
             if r0:
@@ -54,8 +60,8 @@
             parts.append(z)
             parts.append(jnp.zeros((T - r0 - 8, 2 * T), jnp.float32))
             z = jnp.concatenate(parts, axis=0)
-            rest = a_ref[r0 + 8:, :]
-            a_ref[r0 + 8:, :] = rest - lax.dot_general(rest[:, :T], z, NN, precision=HIGHEST, preferred_element_type=jnp.float32)
+            rest = a_ref[r0 + 16:, :]
+            a_ref[r0 + 16:, :] = rest - lax.dot_general(rest[:, :T], z, NN, precision=HIGHEST, preferred_element_type=jnp.float32)
 
 
 def panel_start(j, steps):
@@ -212,64 +218,71 @@
 
     levels = len(orders[0])
     offsets = [[p * rows_of_part] for p in range(len(orders))]
-    size = rows_of_part
-    got_at = 0
+
+    def slot(level, p):
+        half = rows_of_part >> (level + 1)
+        at = (rows_of_part - (rows_of_part >> level)) * len(orders) + p * half
+        return slice(at, at + half)
+
+    def halving(level, p):
+        low, ids = partner(*orders[p][level])
+        half = rows_of_part >> (level + 1)
+        base = offsets[p][level]
+        keep = pl.multiple_of(base + low * half, 8)
+        give = pl.multiple_of(base + (1 - low) * half, 8)
+        offsets[p].append(keep)
+        source = in_ref if level == 0 else sum_ref
+        copy = pltpu.make_async_remote_copy(
+            src_ref=source.at[pl.ds(give, half)], dst_ref=got_ref.at[slot(level, p)],
+            send_sem=send_sems.at[level, p], recv_sem=recv_sems.at[level, p],
+            device_id=ids, device_id_type=pl.DeviceIdType.MESH)
+        copy.start()
+        return copy
+
+    def doubling(level, p):
+        ids = partner(*orders[p][level])[1]
+        region = pl.ds(offsets[p][level + 1], rows_of_part >> (level + 1))
+        copy = pltpu.make_async_remote_copy(
+            src_ref=out_ref.at[region], dst_ref=out_ref.at[region],
+            send_sem=send_sems.at[levels + level, p], recv_sem=recv_sems.at[levels + level, p],
+            device_id=ids, device_id_type=pl.DeviceIdType.MESH)
+        copy.start()
+        return copy
+
+    parts = range(len(orders))
+    flying = [halving(0, p) for p in parts]
     for level in range(levels):
-        half = size // 2
-        sent = []
-        for p, order in enumerate(orders):
-            low, ids = partner(*order[level])
-            base = offsets[p][-1]
-            keep = pl.multiple_of(base + low * half, 8)
-            give = pl.multiple_of(base + (1 - low) * half, 8)
-            slot = got_at + p * half
-            source = in_ref if level == 0 else sum_ref
-            copy = pltpu.make_async_remote_copy(
-                src_ref=source.at[pl.ds(give, half)], dst_ref=got_ref.at[slot:slot + half],
-                send_sem=send_sems.at[level, p], recv_sem=recv_sems.at[level, p],
-                device_id=ids, device_id_type=pl.DeviceIdType.MESH)
-            copy.start()
-            sent.append((copy, keep, slot))
-            offsets[p].append(keep)
-        for copy, keep, slot in sent:
-            copy.wait()
+        for p in parts:
+            flying[p].wait()
             source = in_ref if level == 0 else sum_ref
             target = out_ref if level == levels - 1 else sum_ref
-            target[pl.ds(keep, half), :] = source[pl.ds(keep, half), :] + got_ref[slot:slot + half, :]
-        got_at += half * len(orders)
-        size = half
+            kept = pl.ds(offsets[p][level + 1], rows_of_part >> (level + 1))
+            target[kept, :] = source[kept, :] + got_ref[slot(level, p), :]
+            flying[p] = halving(level + 1, p) if level < levels - 1 else doubling(level, p)
     for level in range(levels - 1, -1, -1):
-        sent = []
-        for p, order in enumerate(orders):
-            low, ids = partner(*order[level])
-            region = pl.ds(offsets[p][level + 1], size)
-            copy = pltpu.make_async_remote_copy(
-                src_ref=out_ref.at[region], dst_ref=out_ref.at[region],
-                send_sem=send_sems.at[levels + level, p], recv_sem=recv_sems.at[levels + level, p],
-                device_id=ids, device_id_type=pl.DeviceIdType.MESH)
-            copy.start()
-            sent.append(copy)
-        for copy in sent:
-            copy.wait()
-        size *= 2
+        for p in parts:
+            flying[p].wait()
+            if level:
+                flying[p] = doubling(level - 1, p)
 
 
 def all_reduce(panels, mesh_sizes):
     sub_bits = [("sub", 1 << b) for b in range(mesh_sizes["sub"].bit_length() - 1)]
     row_bits = [("rows", 1 << b) for b in range(mesh_sizes["rows"].bit_length() - 1)]
     orders = (tuple(sub_bits + row_bits), tuple(sub_bits[:1] + row_bits + sub_bits[1:]))
+    orders = orders + orders
     levels = len(orders[0])
     rows = panels.shape[0]
     return pl.pallas_call(
-        functools.partial(reduce_kernel, orders, rows // 2),
+        functools.partial(reduce_kernel, orders, rows // len(orders)),
         out_shape=jax.ShapeDtypeStruct(panels.shape, jnp.float32),
         in_specs=[VMEM],
         out_specs=VMEM,
         scratch_shapes=[
             pltpu.VMEM(panels.shape, jnp.float32),
             pltpu.VMEM(panels.shape, jnp.float32),
-            pltpu.SemaphoreType.DMA((2 * levels, 2)),
-            pltpu.SemaphoreType.DMA((2 * levels, 2)),
+            pltpu.SemaphoreType.DMA((2 * levels, len(orders))),
+            pltpu.SemaphoreType.DMA((2 * levels, len(orders))),
         ],
         compiler_params=pltpu.CompilerParams(
             collective_id=0, has_side_effects=True, vmem_limit_bytes=24 * 2**20),
@@ -307,7 +320,7 @@
     total_rows = rows_here * devices
     scale = 1.0 / (total_rows * samples.shape[0])
     steps = columns // T
-    unit = 16 * devices
+    unit = 32 * devices
     padded = -(-panel_start(steps, steps) // unit) * unit
     panels = gram_panels(received.reshape(rows_here, columns), counts[None, :], devices, scale, padded)
     return cholesky(all_reduce(panels, mesh_sizes), columns)

time: 180 us -> 156 us (0.87)
  Pallas kernels: 128 us -> 103 us
    pallas_call x1, Pallas kernels: 63.5 us -> 46.1 us  [cholesky(): pl.pallas_call(chol_kernel, out_shape=jax.ShapeDtypeStruct((n, n), jnp.fl...]
    pallas_call x1, Pallas kernels: 54 us -> 47.2 us  [all_reduce(): pl.pallas_call(functools.partial(reduce_kernel, orders, rows // len(order...]
where the time goes in v3:
time: 156 us
  Pallas kernels  103 us (66%)
  waiting for transfers between devices  39.9 us (26%)
  starting transfers between devices  7.52 us (5%)
  local copies, waits for them, and re-layouts  2.91 us (2%)
  other arithmetic  1.7 us (1%)
    pallas_call x1, Pallas kernels, all_reduce(): pl.pallas_call(functools.partial(reduce_kernel, orders, rows // len(order...  47.2 us
    pallas_call x1, Pallas kernels, cholesky(): pl.pallas_call(chol_kernel, out_shape=jax.ShapeDtypeStruct((n, n), jnp.fl...  46.1 us
    all_to_all x1, waiting for transfers between devices, body(): lax.all_to_all(blocks, ('rows', 'sub'), split_axis=0, concat_axis=0, tile...  39.9 us
    pallas_call x1, Pallas kernels, gram_panels(): pl.pallas_call(functools.partial(gram_kernel, mixers, scale), out_shape=j...  8.16 us
    all_to_all x1, starting transfers between devices, body(): lax.all_to_all(blocks, ('rows', 'sub'), split_axis=0, concat_axis=0, tile...  7.52 us
  transfers between devices with their start and end apart: 1, of which 1 were waited for; matrix products, arithmetic and copies ran while one was open for 1% of the time, Pallas kernels for 0%

profile of v3, /device:TPU:0, one launch (start us, length us, event | category | flops | bytes accessed | tf_op | source)
XLA Modules:
  0.0 155.6 jit_solution(17071459504105891184)
XLA Ops:
  0.0 0.7 convert_bitcast_fusion.s_ref
  0.7 0.0 copy-start.1
  0.7 1.6 %copy-done.1 = f32[512,1024]{1,0:T(8,128)S(1)} copy-done((f32[512,1024]{1,0:T(8,128)S(1)}, f32[512,1024]{1,0:T(8,128)}, u32[]{:S(2)}) %copy-start.1) | copy-done | bytes 2097176
  2.3 1.9 %shard_map.37 = f32[512,1024]{1,0:T(8,128)S(1)} custom-call(f32[512,1024]{1,0:T(8,128)S(1)} %copy-done.1, f32[4,128]{1,0:T(4,128)S(1)} %convert_bitcast_fusion.s_ref), custom_call_target="tpu_custom_call" | custom-call | tf_op jit(solution)/shard_map/pallas_call | solution.py:308
  4.2 0.0 copy-start
  4.2 1.3 copy-done
  5.5 0.0 copy-start.2
  5.5 7.5 %all-to-all-start = ((f32[16,32,1024]{2,1,0:T(8,128)}), f32[16,32,1024]{2,1,0:T(8,128)S(1)}, u32[]{:S(2)}, u32[]{:S(2)}) async-start(f32[16,32,1024]{2,1,0:T(8,128)} %bitcast.6), calls=%async_computation | async-start | bytes 4194304 | tf_op jit(solution)/shard_map/all_to_all | solution.py:316
  13.1 0.0 copy-done.2
  13.1 1.0 convert_reduce_fusion
  14.1 39.9 %all-to-all-done = f32[16,32,1024]{2,1,0:T(8,128)S(1)} async-done(((f32[16,32,1024]{2,1,0:T(8,128)}), f32[16,32,1024]{2,1,0:T(8,128)S(1)}, u32[]{:S(2)}, u32[]{:S(2)}) %all-to-all-start) | async-done | bytes 2097184 | tf_op jit(solution)/shard_map/all_to_all | solution.py:316
  54.0 8.2 %shard_map.38.in_ref = f32[4608,128]{1,0:T(8,128)S(1)} custom-call(f32[512,1024]{1,0:T(8,128)S(1)} %bitcast.5, f32[1,512]{1,0:T(1,128)S(1)} %bitcast.7), custom_call_target="tpu_custom_call" | custom-call | tf_op jit(solution)/shard_map/pallas_call | solution.py:194
  62.2 47.2 %shard_map.39.g_in = f32[4608,128]{1,0:T(8,128)S(1)} custom-call(f32[4608,128]{1,0:T(8,128)S(1)} %shard_map.38.in_ref), custom_call_target="tpu_custom_call" | custom-call | tf_op jit(solution)/shard_map/pallas_call | solution.py:276
  109.4 46.1 %shard_map.40 = f32[1024,1024]{1,0:T(8,128)} custom-call(f32[4608,128]{1,0:T(8,128)S(1)} %shard_map.39.g_in), custom_call_target="tpu_custom_call" | custom-call | tf_op jit(solution)/shard_map/pallas_call | solution.py:109
  (1 shorter events, 0.0 us)
Async XLA Ops:
  0.7 1.6 %copy-start.1 = (f32[512,1024]{1,0:T(8,128)S(1)}, f32[512,1024]{1,0:T(8,128)}, u32[]{:S(2)}) copy-start(f32[512,1024]{1,0:T(8,128)} %x_ref.1) | copy-start | bytes 6291460
  4.2 1.3 copy-start
  5.5 7.5 %copy-start.2 = (s32[4096]{0:T(1024)S(1)}, s32[4096]{0:T(1024)}, u32[]{:S(2)}) copy-start(s32[4096]{0:T(1024)} %param.5) | copy-start | bytes 49156
  5.5 48.5 %all-to-all-start = ((f32[16,32,1024]{2,1,0:T(8,128)}), f32[16,32,1024]{2,1,0:T(8,128)S(1)}, u32[]{:S(2)}, u32[]{:S(2)}) async-start(f32[16,32,1024]{2,1,0:T(8,128)} %bitcast.6), calls=%async_computation | async-start | bytes 4194304 | tf_op jit(solution)/shard_map/all_to_all | solution.py:316
